TPU v7x, 128 devices: a whole 4x4x4 slice. The times are simulated.
128 devices in a mesh: rows: 16 (over z, y), cols: 8 (over x, core).
Axes of the slice: x: 4, y: 4, z: 4, core: 2. Of those that a mesh axis runs over, the one named last changes fastest.
Arguments:
- grad_stack: float32 [512, 64, 2048], P(None, 'rows', 'cols'), may hold values from -6 to 6
- moment_stack: float32 [512, 64, 2048], P(None, 'rows', 'cols'), may hold values from -6 to 6
- weight_stack: float32 [512, 64, 2048], P(None, 'rows', 'cols'), may hold values from -0.1875 to 0.1875
Outputs:
- new_weights: float32 [512, 64, 2048], P(None, 'rows', 'cols')
- new_momentum: float32 [512, 64, 2048], P(None, 'rows', 'cols')
All inputs are finite; a program needn't handle non-finite values.
Results may differ from a plain program's by a relative error of at most 0.0003.
Values sent between devices are 32-bit elements.
A program may use at most 128 MiB of HBM per device.

v0:
```python
import jax
import jax.numpy as jnp
from jax import lax
from jax.sharding import PartitionSpec as P

ITERS = 5


hold_rate = 0.95
learn_rate = 1.0


def on_device(grad_stack, moment_stack, weight_stack):
    new_momentum = hold_rate * moment_stack + grad_stack
    moved = lax.all_to_all(new_momentum, "rows", split_axis=0, concat_axis=1, tiled=True)
    whole = lax.all_to_all(moved, "cols", split_axis=0, concat_axis=2, tiled=True)
    iterate = whole * lax.rsqrt(jnp.sum(whole * whole, axis=(1, 2), keepdims=True) + 1e-06)
    for step in range(ITERS):
        gram = jnp.einsum("mik,mjk->mij", iterate, iterate, precision=lax.Precision.HIGHEST)
        mixed = -4.775 * gram + 2.0315 * jnp.einsum(
            "mij,mjk->mik", gram, gram, precision=lax.Precision.HIGHEST
        )
        iterate = 3.4445 * iterate + jnp.einsum(
            "mij,mjk->mik", mixed, iterate, precision=lax.Precision.HIGHEST
        )
    iterate = lax.all_to_all(iterate, "cols", split_axis=2, concat_axis=0, tiled=True)
    back = lax.all_to_all(iterate, "rows", split_axis=1, concat_axis=0, tiled=True)
    new_weights = weight_stack - learn_rate * back
    return (new_weights, new_momentum)


def solution(mesh):
    placed = (P(None, "rows", "cols"), P(None, "rows", "cols"), P(None, "rows", "cols"))
    return jax.shard_map(
        on_device,
        mesh=mesh,
        in_specs=placed,
        out_specs=(P(None, "rows", "cols"), P(None, "rows", "cols")),
        check_vma=False,
    )
```

profile of v0, /device:TPU:0, one launch (start us, length us, event | category | flops | bytes accessed | tf_op | source)
XLA Modules:
  0.0 191.8 jit_solution(6366112335014375146)
XLA Ops:
  0.6 2.9 %multiply_add_fusion = f32[512,4,256]{2,1,0:T(4,128)S(1)} fusion(f32[512,4,256]{2,1,0:T(4,128)} %param.3, f32[512,4,256]{2,1,0:T(4,128)} %param.4), kind=kLoop, calls=%fused_computation.7 | loop fusion | flops 1048576 | bytes 6291456 | tf_op jit(solution)/shard_map/add | solution.py:14
  3.6 37.0 %all_to_all.72 = f32[512,4,256]{2,1,0:T(4,128)S(1)} all-to-all(f32[512,4,256]{2,1,0:T(4,128)S(1)} %multiply_add_fusion), channel_id=1, replica_groups=mesh['rows'=16,'cols'=8] {'rows'}, dimensions={0} | all-to-all | bytes 4194304 | tf_op jit(solution)/shard_map/all_to_all | solution.py:15
  40.6 0.4 copy.29
  41.2 1.2 copy.31
  42.4 31.4 %all_to_all.73 = f32[32,64,256]{2,1,0:T(8,128)S(1)} all-to-all(f32[32,64,256]{2,1,0:T(8,128)S(1)} %copy.31), channel_id=1, replica_groups=mesh['rows'=16,'cols'=8] {'cols'}, dimensions={0} | all-to-all | bytes 4194304 | tf_op jit(solution)/shard_map/all_to_all | solution.py:16
  73.8 0.3 copy.42
  74.1 0.3 multiply_reduce_fusion
  74.4 2.3 %fusion = f32[4,64,64]{2,1,0:T(8,128)S(1)} fusion(f32[4,64,2048]{2,1,0:T(8,128)S(1)} %bitcast.48, f32[4]{0:T(128)S(1)} %add_rsqrt_fusion), kind=kOutput, calls=%fused_computation.8 | convolution fusion | flops 403177472 | bytes 2162704 | tf_op jit(solution)/shard_map/mik,mjk->mij/dot_general | solution.py:19
  77.0 2.1 %convolution_add_fusion.4 = f32[4,64,2048]{2,1,0:T(8,128)S(1)} fusion(f32[4,64,64]{2,1,0:T(8,128)S(1)} %fusion.7, f32[4,64,2048]{2,1,0:T(8,128)S(1)} %bitcast.49, f32[4]{0:T(128)S(1)} %add_rsqrt_fusion), kind=kOutput, calls=%fused_computation.4 | convolution fusion | flops 404750336 | bytes 4259856 | tf_op jit(solution)/shard_map/mij,mjk->mik/dot_general | solution.py:23
  79.1 2.1 %fusion.10 = f32[4,64,64]{2,1,0:T(8,128)S(1)} fusion(f32[4,64,2048]{2,1,0:T(8,128)S(1)} %convolution_add_fusion.4), kind=kOutput, calls=%fused_computation.24 | convolution fusion | flops 402653184 | bytes 2162688 | tf_op jit(solution)/shard_map/mik,mjk->mij/dot_general | solution.py:19
  81.1 0.3 fusion.6
  81.4 2.1 %convolution_add_fusion.3 = f32[4,64,2048]{2,1,0:T(8,128)S(1)} fusion(f32[4,64,64]{2,1,0:T(8,128)S(1)} %fusion.6, f32[4,64,2048]{2,1,0:T(8,128)S(1)} %convolution_add_fusion.4), kind=kOutput, calls=%fused_computation.3 | convolution fusion | flops 403701760 | bytes 4259840 | tf_op jit(solution)/shard_map/mij,mjk->mik/dot_general | solution.py:23
  83.5 2.1 %fusion.11 = f32[4,64,64]{2,1,0:T(8,128)S(1)} fusion(f32[4,64,2048]{2,1,0:T(8,128)S(1)} %convolution_add_fusion.3), kind=kOutput, calls=%fused_computation.25 | convolution fusion | flops 402653184 | bytes 2162688 | tf_op jit(solution)/shard_map/mik,mjk->mij/dot_general | solution.py:19
  85.9 2.3 %convolution_add_fusion.2 = f32[4,64,2048]{2,1,0:T(8,128)S(1)} fusion(f32[4,64,64]{2,1,0:T(8,128)S(1)} %fusion.5, f32[4,64,2048]{2,1,0:T(8,128)S(1)} %convolution_add_fusion.3), kind=kOutput, calls=%fused_computation.2 | convolution fusion | flops 403701760 | bytes 4259840 | tf_op jit(solution)/shard_map/mij,mjk->mik/dot_general | solution.py:23
  88.2 2.1 %fusion.12 = f32[4,64,64]{2,1,0:T(8,128)S(1)} fusion(f32[4,64,2048]{2,1,0:T(8,128)S(1)} %convolution_add_fusion.2), kind=kOutput, calls=%fused_computation.26 | convolution fusion | flops 402653184 | bytes 2162688 | tf_op jit(solution)/shard_map/mik,mjk->mij/dot_general | solution.py:19
  90.3 0.3 fusion.4
  90.6 2.1 %convolution_add_fusion.1 = f32[4,64,2048]{2,1,0:T(8,128)S(1)} fusion(f32[4,64,64]{2,1,0:T(8,128)S(1)} %fusion.4, f32[4,64,2048]{2,1,0:T(8,128)S(1)} %convolution_add_fusion.2), kind=kOutput, calls=%fused_computation.1 | convolution fusion | flops 403701760 | bytes 4259840 | tf_op jit(solution)/shard_map/mij,mjk->mik/dot_general | solution.py:23
  92.7 2.1 %fusion.13 = f32[4,64,64]{2,1,0:T(8,128)S(1)} fusion(f32[4,64,2048]{2,1,0:T(8,128)S(1)} %convolution_add_fusion.1), kind=kOutput, calls=%fused_computation.27 | convolution fusion | flops 402653184 | bytes 2162688 | tf_op jit(solution)/shard_map/mik,mjk->mij/dot_general | solution.py:19
  94.8 0.3 fusion.3
  95.0 2.1 %convolution_add_fusion = f32[4,64,2048]{2,1,0:T(8,128)S(1)} fusion(f32[4,64,64]{2,1,0:T(8,128)S(1)} %fusion.3, f32[4,64,2048]{2,1,0:T(8,128)S(1)} %convolution_add_fusion.1), kind=kOutput, calls=%fused_computation | convolution fusion | flops 403701760 | bytes 4259840 | tf_op jit(solution)/shard_map/mij,mjk->mik/dot_general | solution.py:23
  97.1 3.2 %copy.33 = f32[4,64,2048]{1,0,2:T(4,128)} copy(f32[4,64,2048]{2,1,0:T(8,128)S(1)} %convolution_add_fusion) | data formatting | bytes 4194304 | tf_op jit(solution)/shard_map/add | solution.py:23
  100.3 6.8 %reshape.10 = f32[8,1,65536]{2,1,0:T(1,128)S(1)} reshape(f32[2048,4,64]{2,1,0:T(4,128)} %bitcast.52) | data formatting | bytes 4194304
  107.1 30.7 %all_to_all.74 = f32[8,1,65536]{2,1,0:T(1,128)} all-to-all(f32[8,1,65536]{2,1,0:T(1,128)S(1)} %reshape.10), channel_id=1, replica_groups=mesh['rows'=16,'cols'=8] {'cols'}, dimensions={0} | all-to-all | bytes 4194304 | tf_op jit(solution)/shard_map/all_to_all | solution.py:26
  137.8 0.5 broadcast.37
  138.3 7.2 %reduce.1 = f32[8,65536]{1,0:T(8,128)S(1)} reduce(f32[8,1,65536]{2,1,0:T(1,128)} %all_to_all.74, f32[]{:T(128)} %broadcast.37), dimensions={1}, to_apply=%all_to_all.60.reduce_sub_computation | reduce | bytes 4194308 | tf_op jit(solution)/shard_map/all_to_all | solution.py:26
  145.5 4.8 %reshape.11 = f32[2048,4,64]{2,1,0:T(4,128)} reshape(f32[8,65536]{1,0:T(8,128)S(1)} %reduce.1) | data formatting | bytes 4194304
  150.3 3.5 %copy.41 = f32[4,64,8,256]{3,1,0,2:T(8,128)S(1)} copy(f32[4,64,8,256]{1,0,3,2:T(4,128)} %bitcast.53) | data formatting | bytes 4194304 | tf_op jit(solution)/shard_map/all_to_all | solution.py:26
  153.8 1.2 copy.36
  155.1 31.6 %all_to_all.75 = f32[32,64,256]{2,0,1:T(8,128)S(1)} all-to-all(f32[32,64,256]{2,0,1:T(8,128)S(1)} %copy.36), channel_id=1, replica_groups=mesh['rows'=16,'cols'=8] {'rows'}, dimensions={1} | all-to-all | bytes 4194304 | tf_op jit(solution)/shard_map/all_to_all | solution.py:27
  186.9 1.3 copy-done.1
  188.2 0.4 bitcast_subtract_fusion
  188.7 2.7 %copy.39 = f32[512,4,256]{2,1,0:T(4,128)} copy(f32[512,4,256]{2,0,1:T(8,128)S(1)} %bitcast_subtract_fusion) | data formatting | bytes 4194304
  (8 shorter events, 1.0 us)
Async XLA Ops:
  3.6 37.0 %copy-start = (f32[512,4,256]{2,1,0:T(4,128)}, f32[512,4,256]{2,1,0:T(4,128)S(1)}, u32[]{:S(2)}) copy-start(f32[512,4,256]{2,1,0:T(4,128)S(1)} %multiply_add_fusion) | copy-start | bytes 6291460
  186.6 1.6 copy-start.1
where the time goes:
time: 195 us; the launch traced here: 192 us
  blocking collectives  131 us (67%)
  local copies, waits for them, and re-layouts  26.4 us (14%)
  matrix products  22.6 us (12%)
  other arithmetic  10.9 us (6%)
    all_to_all x1, blocking collectives, on_device(): lax.all_to_all(new_momentum, 'rows', split_axis=0, concat_axis=1, tiled=T...  37 us
    all_to_all x1, blocking collectives, on_device(): lax.all_to_all(iterate, 'rows', split_axis=1, concat_axis=0, tiled=True)  31.6 us
    all_to_all x1, blocking collectives, on_device(): lax.all_to_all(moved, 'cols', split_axis=0, concat_axis=2, tiled=True)  31.4 us
    all_to_all x1, blocking collectives, on_device(): lax.all_to_all(iterate, 'cols', split_axis=2, concat_axis=0, tiled=True)  30.7 us
    unnamed x7, local copies, waits for them, and re-layouts  15.6 us
    dot_general x5, matrix products, on_device(): jnp.einsum('mij,mjk->mik', mixed, iterate, precision=lax.Precision.HIGHEST)  10.7 us
    dot_general x5, matrix products, on_device(): jnp.einsum('mik,mjk->mij', iterate, iterate, precision=lax.Precision.HIGH...  10.6 us
    all_to_all x1, other arithmetic, on_device(): lax.all_to_all(iterate, 'cols', split_axis=2, concat_axis=0, tiled=True)  7.22 us

commit v1 on v0

v1 whole, which is shorter than its diff:
```python
import functools

import jax
import jax.numpy as jnp
from jax import lax
from jax.experimental import pallas as pl
from jax.experimental.pallas import tpu as pltpu
from jax.sharding import PartitionSpec as P

MESH = pl.DeviceIdType.MESH
HIGHEST = lax.Precision.HIGHEST

hold_rate = 0.95
learn_rate = 1.0
ITERS = 5
CHUNKS = 4
BLOCK = 32


def dot(a, b):
    return jnp.dot(a, b, precision=HIGHEST, preferred_element_type=jnp.float32)


def kernel(nm, back, recv, zbuf, obuf, gsend, gx, fsend, frecv, xsend, xrecv, bsend, brecv, local):
    row, col = lax.axis_index("rows"), lax.axis_index("cols")
    z, y = row // 4, row % 4
    x, core = col // 2, col % 2
    mine = core * 16 + row

    def plane_peer(i):
        to_row = ((z + i // 8) % 4) * 4 + (y + (i // 2) % 4) % 4
        to_core = (core + i % 2) % 2
        return to_row, to_core, {"rows": to_row, "cols": x * 2 + to_core}

    def x_peer(i):
        return {"rows": row, "cols": ((x + i) % 4) * 2 + core}

    def part_of(to_row, to_core, chunk):
        return pl.ds(pl.multiple_of((to_row * 2 + to_core) * (CHUNKS * BLOCK) + chunk * BLOCK, BLOCK), BLOCK)

    barrier = pltpu.get_barrier_semaphore()

    def greet(i, carry):
        pl.semaphore_signal(barrier, inc=1, device_id=plane_peer(i)[2], device_id_type=MESH)
        return carry

    def greet_x(i, carry):
        pl.semaphore_signal(barrier, inc=1, device_id=x_peer(i), device_id_type=MESH)
        return carry

    lax.fori_loop(1, 32, greet, 0)
    lax.fori_loop(1, 4, greet_x, 0)
    pl.semaphore_wait(barrier, 34)

    def send_forward(chunk, carry):
        def one(i, carry):
            to_row, to_core, device = plane_peer(i)
            pltpu.make_async_remote_copy(
                src_ref=nm.at[part_of(to_row, to_core, chunk)],
                dst_ref=recv.at[chunk, mine],
                send_sem=fsend,
                recv_sem=frecv.at[chunk],
                device_id=device,
                device_id_type=MESH,
            ).start()
            return carry

        pltpu.make_async_copy(nm.at[part_of(row, core, chunk)], recv.at[chunk, mine], local.at[chunk]).start()
        return lax.fori_loop(1, 32, one, carry)

    lax.fori_loop(0, CHUNKS, send_forward, 0)

    def roll4(v):
        return pltpu.roll(v, 4, 1)

    low = lax.broadcasted_iota(jnp.int32, (16, 8, 128), 1) < 4
    low8 = lax.broadcasted_iota(jnp.int32, (8, 8, 128), 1) < 4
    at_row = lax.broadcasted_iota(jnp.int32, (128, 128), 0)
    at_col = lax.broadcasted_iota(jnp.int32, (128, 128), 1)
    same = (at_row // 4) % 2 == (at_col // 4) % 2
    eye = jnp.where(at_row == at_col, 1.0, 0.0)
    first = (at_row // 4) % 2 == 0

    def grams(chunk):
        pltpu.make_async_copy(recv.at[chunk, pl.ds(0, 31)], recv.at[chunk, pl.ds(0, 31)], frecv.at[chunk]).wait()
        pltpu.make_async_copy(recv.at[chunk, 0], recv.at[chunk, 0], local.at[chunk]).wait()
        for pair in range(2):
            blocks = []
            for k in range(2):
                a = recv[chunk, 16 * k : 16 * k + 16, 16 * pair : 16 * pair + 8, :]
                b = recv[chunk, 16 * k : 16 * k + 16, 16 * pair + 8 : 16 * pair + 16, :]
                blocks.append(jnp.where(low, a, roll4(b)).reshape(128, 128))
                blocks.append(jnp.where(low, roll4(a), b).reshape(128, 128))
            whole = jnp.concatenate(blocks, axis=1)
            zbuf[chunk, pair] = whole
            gram = lax.dot_general(
                whole, whole, (((1,), (1,)), ((), ())), precision=HIGHEST, preferred_element_type=jnp.float32
            )
            gram = jnp.where(same, gram, 0.0).reshape(8, 2, 8, 128)
            even, odd = gram[:, 0], gram[:, 1]
            even, odd = even + roll4(even), odd + roll4(odd)
            gsend[chunk, 64 * pair : 64 * pair + 64, :] = jnp.where(low8, even, odd).reshape(64, 128)

        def one(i, carry):
            pltpu.make_async_remote_copy(
                src_ref=gsend.at[chunk],
                dst_ref=gx.at[chunk, x],
                send_sem=xsend,
                recv_sem=xrecv.at[chunk],
                device_id=x_peer(i),
                device_id_type=MESH,
            ).start()
            return carry

        lax.fori_loop(1, 4, one, 0)
        gx[chunk, x] = gsend[chunk]

    def finish(chunk):
        pltpu.make_async_copy(gx.at[chunk, pl.ds(0, 3)], gx.at[chunk, pl.ds(0, 3)], xrecv.at[chunk]).wait()
        total = (gx[chunk, 0] + gx[chunk, 1]) + (gx[chunk, 2] + gx[chunk, 3])
        state = []
        for pair in range(2):
            part = total[64 * pair : 64 * pair + 64].reshape(8, 8, 128)
            turned = roll4(part)
            gram = jnp.stack([jnp.where(low8, part, turned), jnp.where(low8, turned, part)], axis=1).reshape(128, 128)
            gram = jnp.where(same, gram, 0.0)
            diag = gram * eye
            one = jnp.sum(jnp.where(first, diag, 0.0), keepdims=True) + 1e-06
            two = jnp.sum(jnp.where(first, 0.0, diag), keepdims=True) + 1e-06
            norm = jnp.where(first, one, two)
            scale = lax.rsqrt(norm)
            state.append([gram * scale * scale, None, scale])
        for step in range(ITERS):
            for one in state:
                gram, total_map, scale = one
                square = dot(gram, gram)
                mixed = 3.4445 * eye - 4.775 * gram + 2.0315 * square
                one[1] = mixed if total_map is None else dot(mixed, total_map)
                if step < ITERS - 1:
                    one[0] = dot(dot(mixed, gram), mixed)
        for pair in range(2):
            out = dot(state[pair][1] * state[pair][2], zbuf[chunk, pair])
            for k in range(2):
                c0 = out[:, 256 * k : 256 * k + 128].reshape(16, 8, 128)
                c1 = out[:, 256 * k + 128 : 256 * k + 256].reshape(16, 8, 128)
                obuf[chunk, 16 * k : 16 * k + 16, 16 * pair : 16 * pair + 8, :] = jnp.where(low, c0, roll4(c1))
                obuf[chunk, 16 * k : 16 * k + 16, 16 * pair + 8 : 16 * pair + 16, :] = jnp.where(low, roll4(c0), c1)

        def one(i, carry):
            to_row, to_core, device = plane_peer(i)
            pltpu.make_async_remote_copy(
                src_ref=obuf.at[chunk, to_core * 16 + to_row],
                dst_ref=back.at[part_of(row, core, chunk)],
                send_sem=bsend,
                recv_sem=brecv,
                device_id=device,
                device_id_type=MESH,
            ).start()
            return carry

        lax.fori_loop(1, 32, one, 0)
        pltpu.make_async_copy(obuf.at[chunk, mine], back.at[part_of(row, core, chunk)], local.at[CHUNKS]).start()

    def step(t, carry):
        @pl.when(t < CHUNKS)
        def _():
            grams(t)

        @pl.when(t > 0)
        def _():
            finish(t - 1)

        return carry

    lax.fori_loop(0, CHUNKS + 1, step, 0)

    def drain(sem, ref):
        pltpu.make_async_copy(ref, ref, sem).wait()

    away = pl.ds(0, 31 * CHUNKS * BLOCK)
    drain(brecv, back.at[away])
    drain(local.at[CHUNKS], back.at[pl.ds(0, CHUNKS * BLOCK)])
    drain(fsend, back.at[away])
    drain(bsend, back.at[away])
    drain(xsend, gx.at[pl.ds(0, 3)])


def exchange(nm):
    f32 = jnp.float32
    return pl.pallas_call(
        kernel,
        out_shape=jax.ShapeDtypeStruct((4096, 128), f32),
        in_specs=[pl.BlockSpec(memory_space=pltpu.VMEM)],
        out_specs=pl.BlockSpec(memory_space=pltpu.VMEM),
        scratch_shapes=[
            pltpu.VMEM((CHUNKS, 32, BLOCK, 128), f32),
            pltpu.VMEM((CHUNKS, 2, 128, 512), f32),
            pltpu.VMEM((CHUNKS, 32, BLOCK, 128), f32),
            pltpu.VMEM((CHUNKS, 128, 128), f32),
            pltpu.VMEM((CHUNKS, 4, 128, 128), f32),
            pltpu.SemaphoreType.DMA,
            pltpu.SemaphoreType.DMA((CHUNKS,)),
            pltpu.SemaphoreType.DMA,
            pltpu.SemaphoreType.DMA((CHUNKS,)),
            pltpu.SemaphoreType.DMA,
            pltpu.SemaphoreType.DMA,
            pltpu.SemaphoreType.DMA((CHUNKS + 1,)),
        ],
        compiler_params=pltpu.CompilerParams(collective_id=0, has_side_effects=True, vmem_limit_bytes=40 * 1024 * 1024),
        name="exchange",
    )(nm)


def flat(a):
    return a.reshape(512, 4, 2, 128).transpose(0, 2, 1, 3).reshape(4096, 128)


def unflat(a):
    return a.reshape(512, 2, 4, 128).transpose(0, 2, 1, 3).reshape(512, 4, 256)


def on_device(grad_stack, moment_stack, weight_stack):
    new_momentum = hold_rate * moment_stack + grad_stack
    back = unflat(exchange(flat(new_momentum)))
    new_weights = weight_stack - learn_rate * back
    return (new_weights, new_momentum)


def solution(mesh):
    placed = (P(None, "rows", "cols"), P(None, "rows", "cols"), P(None, "rows", "cols"))
    return jax.shard_map(
        on_device,
        mesh=mesh,
        in_specs=placed,
        out_specs=(P(None, "rows", "cols"), P(None, "rows", "cols")),
        check_vma=False,
    )
```

time: 195 us -> 68.4 us (0.35); the launches traced: 192 us -> 67.8 us
  blocking collectives: 131 us -> 0 us
  Pallas kernels: 0 us -> 62.3 us
  local copies, waits for them, and re-layouts: 26.4 us -> 0.01 us
  matrix products: 22.6 us -> 0 us
  other arithmetic: 10.9 us -> 4.8 us
    all_to_all x4 -> x0, blocking collectives: 131 us -> none  [the longest x1 37 us: on_device(): lax.all_to_all(new_momentum, 'rows', split_axis=0, concat_axis=1, tiled=T...]
    pallas_call x0 -> x1, Pallas kernels: none -> 62.3 us  [exchange(): pl.pallas_call(kernel, out_shape=jax.ShapeDtypeStruct((4096, 128), f32),...]
    dot_general x15 -> x0, matrix products: 22.6 us -> none  [the longest x5 10.7 us: on_device(): jnp.einsum('mij,mjk->mik', mixed, iterate, precision=lax.Precision.HIGHEST)]
    unnamed x7 -> x4, local copies, waits for them, and re-layouts: 15.6 us -> 0.01 us
    all_to_all x8 -> x0, local copies, waits for them, and re-layouts: 7.61 us -> none  [the longest x3 5.24 us: on_device(): lax.all_to_all(iterate, 'cols', split_axis=2, concat_axis=0, tiled=True)]
    all_to_all x1 -> x0, other arithmetic: 7.22 us -> none  [on_device(): lax.all_to_all(iterate, 'cols', split_axis=2, concat_axis=0, tiled=True)]
    add x1 -> x0, local copies, waits for them, and re-layouts: 3.17 us -> none  [on_device(): 3.4445 * iterate]
where the time goes in v1:
time: 68.4 us; the launch traced here: 67.8 us
  Pallas kernels  62.3 us (91%)
  other arithmetic  4.8 us (7%)
    pallas_call x1, Pallas kernels, exchange(): pl.pallas_call(kernel, out_shape=jax.ShapeDtypeStruct((4096, 128), f32),...  62.3 us
    add x1, other arithmetic, on_device(): new_momentum = hold_rate * moment_stack + grad_stack  2.94 us
    sub x1, other arithmetic, on_device(): new_weights = weight_stack - learn_rate * back  1.86 us

profile of v1, /device:TPU:0, one launch (start us, length us, event | category | flops | bytes accessed | tf_op | source)
XLA Modules:
  0.0 67.8 jit_solution(8484362598420017733)
XLA Ops:
  0.6 2.9 %multiply_add_fusion = f32[512,4,256]{2,1,0:T(4,128)S(1)} fusion(f32[512,4,256]{2,1,0:T(4,128)} %param.3, f32[512,4,256]{2,1,0:T(4,128)} %param.4), kind=kLoop, calls=%fused_computation | loop fusion | flops 1048576 | bytes 6291456 | tf_op jit(solution)/shard_map/add | solution.py:223
  3.6 0.0 copy-start
  3.6 0.0 copy-start.1
  3.6 62.3 %exchange.1 = f32[4096,128]{1,0:T(8,128)S(1)} custom-call(f32[4096,128]{1,0:T(8,128)S(1)} %bitcast.10), custom_call_target="tpu_custom_call" | custom-call | tf_op jit(solution)/shard_map/exchange/pallas_call | solution.py:190
  65.9 0.0 copy-done
  65.9 0.0 copy-done.1
  65.9 1.9 %sub.3 = f32[512,4,256]{2,1,0:T(4,128)} subtract(f32[512,4,256]{2,1,0:T(4,128)S(1)} %copy-done.1, f32[512,4,256]{2,1,0:T(4,128)S(1)} %bitcast.11) | non-fusion elementwise | flops 524288 | bytes 6291456 | tf_op jit(solution)/shard_map/sub | solution.py:225
Async XLA Ops:
  3.6 62.3 %copy-start = (f32[512,4,256]{2,1,0:T(4,128)}, f32[512,4,256]{2,1,0:T(4,128)S(1)}, u32[]{:S(2)}) copy-start(f32[512,4,256]{2,1,0:T(4,128)S(1)} %multiply_add_fusion) | copy-start | bytes 6291460
  3.6 62.3 %copy-start.1 = (f32[512,4,256]{2,1,0:T(4,128)S(1)}, f32[512,4,256]{2,1,0:T(4,128)}, u32[]{:S(2)}) copy-start(f32[512,4,256]{2,1,0:T(4,128)} %param.5) | copy-start | bytes 6291460

commit v2 on v0

v2 whole, which is shorter than its diff:
```python
import jax
import jax.numpy as jnp
from jax import lax
from jax.experimental import pallas as pl
from jax.experimental.pallas import tpu as pltpu
from jax.sharding import PartitionSpec as P

MESH = pl.DeviceIdType.MESH
HIGHEST = lax.Precision.HIGHEST

hold_rate = 0.95
learn_rate = 1.0
ITERS = 5
CHUNKS = 4


def dot(a, b):
    return jnp.dot(a, b, precision=HIGHEST, preferred_element_type=jnp.float32)


def kernel(
    grad, moment, weight, momentum, result,
    gbuf, mbuf, wbuf, out1, in1, in2, zbuf, out2, in3, in4, gsend, gx,
    load, wload, local, send, recv1, recv2, recv3, recv4, xrecv,
):
    row, col = lax.axis_index("rows"), lax.axis_index("cols")
    z, y = row // 4, row % 4
    x, core = col // 2, col % 2
    first, second = (y, z), (z, y)

    def along_first(half, i):
        to = (first[half] + i) % 4
        to_row = z * 4 + to if half == 0 else to * 4 + y
        return to, {"rows": to_row, "cols": col}

    def along_second(half, i):
        to, to_core = (second[half] + i // 2) % 4, (core + i % 2) % 2
        to_row = to * 4 + y if half == 0 else z * 4 + to
        return to, to_core, {"rows": to_row, "cols": x * 2 + to_core}

    def x_peer(i):
        return {"rows": row, "cols": ((x + i) % 4) * 2 + core}

    def loop(start, stop, body):
        def one(i, carry):
            body(i)
            return carry

        lax.fori_loop(start, stop, one, 0)

    barrier = pltpu.get_barrier_semaphore()

    def greet(device):
        pl.semaphore_signal(barrier, inc=1, device_id=device, device_id_type=MESH)

    for chunk in range(CHUNKS):
        pltpu.make_async_copy(grad.at[:, chunk], gbuf.at[:, chunk], load.at[chunk]).start()
        pltpu.make_async_copy(moment.at[:, chunk], mbuf.at[:, chunk], load.at[CHUNKS + chunk]).start()
    greet({"rows": row, "cols": x * 2 + (core + 1) % 2})
    loop(2, 8, lambda i: greet(along_second(0, i)[2]))
    loop(2, 8, lambda i: greet(along_second(1, i)[2]))
    loop(1, 4, lambda i: greet(x_peer(i)))

    def remote(src, dst, sem, device, which):
        pltpu.make_async_remote_copy(
            src_ref=src, dst_ref=dst, send_sem=send.at[which], recv_sem=sem, device_id=device, device_id_type=MESH
        ).start()

    def drain(ref, sem):
        pltpu.make_async_copy(ref, ref, sem).wait()

    def new_momentum(chunk):
        pltpu.make_async_copy(grad.at[:, chunk], gbuf.at[:, chunk], load.at[chunk]).wait()
        pltpu.make_async_copy(moment.at[:, chunk], mbuf.at[:, chunk], load.at[CHUNKS + chunk]).wait()
        for home in range(32):
            to_z, to_y, to_core = home // 8, (home // 2) % 4, home % 2
            value = hold_rate * mbuf[home, chunk] + gbuf[home, chunk]
            momentum[home, chunk] = value
            out1[chunk, 0, to_y, to_z * 2 + to_core] = value[:16]
            out1[chunk, 1, to_z, to_y * 2 + to_core] = value[16:]

    def send1(chunk):
        for half in range(2):
            own = first[half]
            pltpu.make_async_copy(out1.at[chunk, half, own], in1.at[chunk, half, :, own], local.at[chunk]).start()

        def one(i):
            for half in range(2):
                to, device = along_first(half, i)
                remote(out1.at[chunk, half, to], in1.at[chunk, half, :, first[half]], recv1.at[chunk], device, 0)

        loop(1, 4, one)

    def send2(chunk):
        drain(out1.at[chunk, :, pl.ds(0, 3)], recv1.at[chunk])
        drain(out1.at[chunk, :, 0], local.at[chunk])
        for half in range(2):
            pltpu.make_async_copy(
                in1.at[chunk, half, second[half] * 2 + core],
                in2.at[chunk, half, core * 4 + second[half]],
                local.at[CHUNKS + chunk],
            ).start()

        def one(i):
            for half in range(2):
                to, to_core, device = along_second(half, i)
                remote(
                    in1.at[chunk, half, to * 2 + to_core],
                    in2.at[chunk, half, core * 4 + second[half]],
                    recv2.at[chunk],
                    device,
                    1,
                )

        loop(1, 8, one)

    def send3(chunk):
        for half in range(2):
            pltpu.make_async_copy(
                out2.at[chunk, half, core * 4 + second[half]],
                in3.at[chunk, half, :, second[half] * 2 + core],
                local.at[2 * CHUNKS + chunk],
            ).start()

        def one(i):
            for half in range(2):
                to, to_core, device = along_second(half, i)
                remote(
                    out2.at[chunk, half, to_core * 4 + to],
                    in3.at[chunk, half, :, second[half] * 2 + core],
                    recv3.at[chunk],
                    device,
                    2,
                )

        loop(1, 8, one)

    def send4(chunk):
        drain(out2.at[chunk, :, pl.ds(0, 7)], recv3.at[chunk])
        drain(out2.at[chunk, :, 0], local.at[2 * CHUNKS + chunk])
        for half in range(2):
            own = first[half]
            pltpu.make_async_copy(in3.at[chunk, half, own], in4.at[chunk, half, own], local.at[3 * CHUNKS + chunk]).start()

        def one(i):
            for half in range(2):
                to, device = along_first(half, i)
                remote(in3.at[chunk, half, to], in4.at[chunk, half, first[half]], recv4.at[chunk], device, 3)

        loop(1, 4, one)

    def subtract(chunk):
        drain(in4.at[chunk, :, pl.ds(0, 3)], recv4.at[chunk])
        drain(in4.at[chunk, :, 0], local.at[3 * CHUNKS + chunk])
        for home in range(32):
            to_z, to_y, to_core = home // 8, (home // 2) % 4, home % 2
            result[home, chunk, :16] = wbuf[home, chunk, :16] - learn_rate * in4[chunk, 0, to_y, to_z * 2 + to_core]
            result[home, chunk, 16:] = wbuf[home, chunk, 16:] - learn_rate * in4[chunk, 1, to_z, to_y * 2 + to_core]

    def roll4(v):
        return pltpu.roll(v, 4, 1)

    low = lax.broadcasted_iota(jnp.int32, (16, 8, 128), 1) < 4
    low8 = lax.broadcasted_iota(jnp.int32, (8, 8, 128), 1) < 4
    at_row = lax.broadcasted_iota(jnp.int32, (128, 128), 0)
    at_col = lax.broadcasted_iota(jnp.int32, (128, 128), 1)
    same = (at_row // 4) % 2 == (at_col // 4) % 2
    eye = jnp.where(at_row == at_col, 1.0, 0.0)
    upper = (at_row // 4) % 2 == 0

    def grams(chunk):
        drain(in2.at[chunk, :, pl.ds(0, 7)], recv2.at[chunk])
        drain(in2.at[chunk, :, 0], local.at[CHUNKS + chunk])
        for half in range(2):
            blocks = []
            for k in range(2):
                both = in2[chunk, half, 4 * k : 4 * k + 4].reshape(16, 16, 128)
                a, b = both[:, :8], both[:, 8:]
                blocks.append(jnp.where(low, a, roll4(b)).reshape(128, 128))
                blocks.append(jnp.where(low, roll4(a), b).reshape(128, 128))
            whole = jnp.concatenate(blocks, axis=1)
            zbuf[chunk, half] = whole
            gram = lax.dot_general(
                whole, whole, (((1,), (1,)), ((), ())), precision=HIGHEST, preferred_element_type=jnp.float32
            )
            gram = jnp.where(same, gram, 0.0).reshape(8, 2, 8, 128)
            even, odd = gram[:, 0], gram[:, 1]
            even, odd = even + roll4(even), odd + roll4(odd)
            gsend[chunk, 64 * half : 64 * half + 64, :] = jnp.where(low8, even, odd).reshape(64, 128)
        loop(1, 4, lambda i: remote(gsend.at[chunk], gx.at[chunk, x], xrecv.at[chunk], x_peer(i), 4))
        gx[chunk, x] = gsend[chunk]

    def iterate(chunk):
        drain(gx.at[chunk, pl.ds(0, 3)], xrecv.at[chunk])
        total = (gx[chunk, 0] + gx[chunk, 1]) + (gx[chunk, 2] + gx[chunk, 3])
        state = []
        for half in range(2):
            part = total[64 * half : 64 * half + 64].reshape(8, 8, 128)
            turned = roll4(part)
            gram = jnp.stack([jnp.where(low8, part, turned), jnp.where(low8, turned, part)], axis=1).reshape(128, 128)
            gram = jnp.where(same, gram, 0.0)
            diag = gram * eye
            one = jnp.sum(jnp.where(upper, diag, 0.0), keepdims=True) + 1e-06
            two = jnp.sum(jnp.where(upper, 0.0, diag), keepdims=True) + 1e-06
            scale = lax.rsqrt(jnp.where(upper, one, two))
            state.append([gram * scale * scale, None, scale])
        for step in range(ITERS):
            for one in state:
                gram, product, scale = one
                mixed = 3.4445 * eye - 4.775 * gram + 2.0315 * dot(gram, gram)
                one[1] = mixed if product is None else dot(mixed, product)
                if step < ITERS - 1:
                    one[0] = dot(dot(mixed, gram), mixed)
        return [product * scale for _, product, scale in state]

    def apply(chunk, products):
        for half in range(2):
            out = dot(products[half], zbuf[chunk, half])
            for k in range(2):
                c0 = out[:, 256 * k : 256 * k + 128].reshape(16, 8, 128)
                c1 = out[:, 256 * k + 128 : 256 * k + 256].reshape(16, 8, 128)
                a, b = jnp.where(low, c0, roll4(c1)), jnp.where(low, roll4(c0), c1)
                out2[chunk, half, 4 * k : 4 * k + 4] = jnp.concatenate([a, b], axis=1).reshape(4, 4, 16, 128)

    new_momentum(0)
    pl.semaphore_wait(barrier, 16)
    send1(0)
    new_momentum(1)
    send1(1)
    new_momentum(2)
    new_momentum(3)
    pltpu.make_async_copy(weight, wbuf, wload).start()
    send2(0)
    send1(2)
    send2(1)
    send1(3)
    grams(0)
    send2(2)
    grams(1)

    def step(t):
        products = iterate(t)

        @pl.when(t == 0)
        def _():
            send2(3)

        apply(t, products)
        send3(t)

        @pl.when(t < 2)
        def _():
            grams(t + 2)

        @pl.when(t > 0)
        def _():
            send4(t - 1)

    loop(0, CHUNKS, step)
    send4(3)
    pltpu.make_async_copy(weight, wbuf, wload).wait()
    loop(0, CHUNKS, subtract)

    drain(out1.at[:, :, pl.ds(0, 3)], send.at[0])
    drain(out2.at[:, :, pl.ds(0, 7)], send.at[1])
    drain(out2.at[:, :, pl.ds(0, 7)], send.at[2])
    drain(out1.at[:, :, pl.ds(0, 3)], send.at[3])
    drain(gx.at[:, pl.ds(0, 3)], send.at[4])


def update(grad, moment, weight):
    f32 = jnp.float32
    whole = (32, CHUNKS, 32, 128)
    by_first = (CHUNKS, 2, 4, 8, 16, 128)
    by_second = (CHUNKS, 2, 8, 4, 16, 128)
    dma = pltpu.SemaphoreType.DMA
    return pl.pallas_call(
        kernel,
        out_shape=[jax.ShapeDtypeStruct(whole, f32)] * 2,
        in_specs=[pl.BlockSpec(memory_space=pltpu.HBM)] * 3,
        out_specs=[pl.BlockSpec(memory_space=pltpu.VMEM)] * 2,
        scratch_shapes=[
            pltpu.VMEM(whole, f32),
            pltpu.VMEM(whole, f32),
            pltpu.VMEM(whole, f32),
            pltpu.VMEM(by_first, f32),
            pltpu.VMEM(by_second, f32),
            pltpu.VMEM(by_second, f32),
            pltpu.VMEM((CHUNKS, 2, 128, 512), f32),
            pltpu.VMEM(by_second, f32),
            pltpu.VMEM(by_first, f32),
            pltpu.VMEM(by_first, f32),
            pltpu.VMEM((CHUNKS, 128, 128), f32),
            pltpu.VMEM((CHUNKS, 4, 128, 128), f32),
            dma((2 * CHUNKS,)),
            dma,
            dma((4 * CHUNKS,)),
            dma((5,)),
            dma((CHUNKS,)),
            dma((CHUNKS,)),
            dma((CHUNKS,)),
            dma((CHUNKS,)),
            dma((CHUNKS,)),
        ],
        compiler_params=pltpu.CompilerParams(collective_id=0, has_side_effects=True, vmem_limit_bytes=61000000),
        name="update",
    )(grad, moment, weight)


def tiles(a):
    return a.reshape(512, 4, 2, 128).transpose(0, 2, 1, 3).reshape(32, CHUNKS, 32, 128)


def untiled(a):
    return a.reshape(512, 2, 4, 128).transpose(0, 2, 1, 3).reshape(512, 4, 256)


def on_device(grad_stack, moment_stack, weight_stack):
    momentum, result = update(tiles(grad_stack), tiles(moment_stack), tiles(weight_stack))
    return (untiled(result), untiled(momentum))


def solution(mesh):
    placed = (P(None, "rows", "cols"), P(None, "rows", "cols"), P(None, "rows", "cols"))
    return jax.shard_map(
        on_device,
        mesh=mesh,
        in_specs=placed,
        out_specs=(P(None, "rows", "cols"), P(None, "rows", "cols")),
        check_vma=False,
    )
```

time: 195 us -> 68.1 us (0.35); the launches traced: 192 us -> 67 us
  blocking collectives: 131 us -> 0 us
  Pallas kernels: 0 us -> 61.6 us
  matrix products: 22.6 us -> 0 us
  local copies, waits for them, and re-layouts: 26.4 us -> 4.74 us
  other arithmetic: 10.9 us -> 0 us
    all_to_all x4 -> x0, blocking collectives: 131 us -> none  [the longest x1 37 us: on_device(): lax.all_to_all(new_momentum, 'rows', split_axis=0, concat_axis=1, tiled=T...]
    pallas_call x0 -> x1, Pallas kernels: none -> 61.6 us  [update(): pl.pallas_call(kernel, out_shape=[jax.ShapeDtypeStruct(whole, f32)] * 2,...]
    dot_general x15 -> x0, matrix products: 22.6 us -> none  [the longest x5 10.7 us: on_device(): jnp.einsum('mij,mjk->mik', mixed, iterate, precision=lax.Precision.HIGHEST)]
    unnamed x7 -> x4, local copies, waits for them, and re-layouts: 15.6 us -> 4.74 us
    all_to_all x8 -> x0, local copies, waits for them, and re-layouts: 7.61 us -> none  [the longest x3 5.24 us: on_device(): lax.all_to_all(iterate, 'cols', split_axis=2, concat_axis=0, tiled=True)]
    all_to_all x1 -> x0, other arithmetic: 7.22 us -> none  [on_device(): lax.all_to_all(iterate, 'cols', split_axis=2, concat_axis=0, tiled=True)]
    add x1 -> x0, local copies, waits for them, and re-layouts: 3.17 us -> none  [on_device(): 3.4445 * iterate]
    add x1 -> x0, other arithmetic: 2.94 us -> none  [on_device(): new_momentum = hold_rate * moment_stack + grad_stack]
where the time goes in v2:
time: 68.1 us; the launch traced here: 67 us
  Pallas kernels  61.6 us (90%)
  local copies, waits for them, and re-layouts  4.74 us (7%)
    pallas_call x1, Pallas kernels, update(): pl.pallas_call(kernel, out_shape=[jax.ShapeDtypeStruct(whole, f32)] * 2,...  61.6 us
    unnamed x4, local copies, waits for them, and re-layouts  4.74 us

profile of v2, /device:TPU:0, one launch (start us, length us, event | category | flops | bytes accessed | tf_op | source)
XLA Modules:
  0.0 67.0 jit_solution(1358343819365234478)
XLA Ops:
  0.6 61.6 %update.1 = (f32[32,4,32,128]{3,2,1,0:T(8,128)}, f32[32,4,32,128]{3,2,1,0:T(8,128)}) custom-call(f32[32,4,32,128]{3,2,1,0:T(8,128)} %bitcast.25, f32[32,4,32,128]{3,2,1,0:T(8,128)} %bitcast.26, f32[32,4,32,128]{3,2,1,0:T(8,128)} %bitcast.27), custom_call_target="tpu_custom_call" | custom-call | tf_op jit(solution)/shard_map/update/pallas_call | solution.py:277
  62.3 0.0 copy-start
  62.3 3.4 %copy.12 = f32[512,4,256]{2,1,0:T(4,128)} copy(f32[512,4,256]{2,1,0:T(4,128)} %bitcast.29) | data formatting | bytes 4194304
  65.7 0.0 copy-done
  65.7 1.3 %copy.13 = f32[512,4,256]{2,1,0:T(4,128)} copy(f32[512,4,256]{2,1,0:T(4,128)S(1)} %bitcast.28) | data formatting | bytes 4194304
Async XLA Ops:
  62.3 3.4 %copy-start = (f32[32,4,32,128]{3,2,1,0:T(8,128)S(1)}, f32[32,4,32,128]{3,2,1,0:T(8,128)}, u32[]{:S(2)}) copy-start(f32[32,4,32,128]{3,2,1,0:T(8,128)} %get-tuple-element.5) | copy-start | bytes 6291460

commit v3 on v2

--- a/solution.py
+++ b/solution.py
@@ -14,8 +14,25 @@
 CHUNKS = 4
 
 
-def dot(a, b):
-    return jnp.dot(a, b, precision=HIGHEST, preferred_element_type=jnp.float32)
+def split(a):
+    high = a.astype(jnp.bfloat16)
+    rest = a - high.astype(jnp.float32)
+    middle = rest.astype(jnp.bfloat16)
+    return high, middle, (rest - middle.astype(jnp.float32)).astype(jnp.bfloat16)
+
+
+def dot6(a, b):
+    (ah, am, al), (bh, bm, bl) = a, b
+    n = bh.shape[1]
+    wide, small = jnp.concatenate([ah, am], axis=1), jnp.concatenate([ah, al], axis=1)
+    top, middle = jnp.concatenate([bh, bh], axis=0), jnp.concatenate([bm, bm], axis=0)
+    rest = jnp.dot(small, jnp.concatenate([bl, bh], axis=0), preferred_element_type=jnp.float32)
+    if n > 128:
+        return (rest + jnp.dot(wide, middle, preferred_element_type=jnp.float32)) + jnp.dot(
+            wide, top, preferred_element_type=jnp.float32
+        )
+    both = jnp.dot(wide, jnp.concatenate([top, middle], axis=1), preferred_element_type=jnp.float32)
+    return (rest + both[:, n:]) + both[:, :n]
 
 
 def kernel(
@@ -89,7 +106,8 @@
                 to, device = along_first(half, i)
                 remote(out1.at[chunk, half, to], in1.at[chunk, half, :, first[half]], recv1.at[chunk], device, 0)
 
-        loop(1, 4, one)
+        for i in (2, 1, 3):
+            one(i)
 
     def send2(chunk):
         drain(out1.at[chunk, :, pl.ds(0, 3)], recv1.at[chunk])
@@ -112,7 +130,8 @@
                     1,
                 )
 
-        loop(1, 8, one)
+        for i in (4, 5, 2, 3, 6, 7, 1):
+            one(i)
 
     def send3(chunk):
         for half in range(2):
@@ -133,7 +152,8 @@
                     2,
                 )
 
-        loop(1, 8, one)
+        for i in (4, 5, 2, 3, 6, 7, 1):
+            one(i)
 
     def send4(chunk):
         drain(out2.at[chunk, :, pl.ds(0, 7)], recv3.at[chunk])
@@ -147,7 +167,8 @@
                 to, device = along_first(half, i)
                 remote(in3.at[chunk, half, to], in4.at[chunk, half, first[half]], recv4.at[chunk], device, 3)
 
-        loop(1, 4, one)
+        for i in (2, 1, 3):
+            one(i)
 
     def subtract(chunk):
         drain(in4.at[chunk, :, pl.ds(0, 3)], recv4.at[chunk])
@@ -187,7 +208,8 @@
             even, odd = gram[:, 0], gram[:, 1]
             even, odd = even + roll4(even), odd + roll4(odd)
             gsend[chunk, 64 * half : 64 * half + 64, :] = jnp.where(low8, even, odd).reshape(64, 128)
-        loop(1, 4, lambda i: remote(gsend.at[chunk], gx.at[chunk, x], xrecv.at[chunk], x_peer(i), 4))
+        for i in (2, 1, 3):
+            remote(gsend.at[chunk], gx.at[chunk, x], xrecv.at[chunk], x_peer(i), 4)
         gx[chunk, x] = gsend[chunk]
 
     def iterate(chunk):
@@ -204,18 +226,26 @@
             two = jnp.sum(jnp.where(upper, 0.0, diag), keepdims=True) + 1e-06
             scale = lax.rsqrt(jnp.where(upper, one, two))
             state.append([gram * scale * scale, None, scale])
+        grams_now, scales = [one[0] for one in state], [one[2] for one in state]
+        products = None
         for step in range(ITERS):
-            for one in state:
-                gram, product, scale = one
-                mixed = 3.4445 * eye - 4.775 * gram + 2.0315 * dot(gram, gram)
-                one[1] = mixed if product is None else dot(mixed, product)
-                if step < ITERS - 1:
-                    one[0] = dot(dot(mixed, gram), mixed)
-        return [product * scale for _, product, scale in state]
+            parts = [split(v) for v in grams_now]
+            squares = [dot6(p, p) for p in parts]
+            mixed = [3.4445 * eye - 4.775 * g + 2.0315 * s for g, s in zip(grams_now, squares)]
+            mixed_parts = [split(v) for v in mixed]
+            if step < ITERS - 1:
+                turned = [dot6(m, p) for m, p in zip(mixed_parts, parts)]
+            if products is None:
+                products = mixed
+            else:
+                products = [dot6(m, split(p)) for m, p in zip(mixed_parts, products)]
+            if step < ITERS - 1:
+                grams_now = [dot6(split(t), m) for t, m in zip(turned, mixed_parts)]
+        return [split(product * scale) for product, scale in zip(products, scales)]
 
     def apply(chunk, products):
         for half in range(2):
-            out = dot(products[half], zbuf[chunk, half])
+            out = dot6(products[half], split(zbuf[chunk, half]))
             for k in range(2):
                 c0 = out[:, 256 * k : 256 * k + 128].reshape(16, 8, 128)
                 c1 = out[:, 256 * k + 128 : 256 * k + 256].reshape(16, 8, 128)
@@ -231,12 +261,12 @@
     new_momentum(3)
     pltpu.make_async_copy(weight, wbuf, wload).start()
     send2(0)
+    send2(1)
     send1(2)
-    send2(1)
+    grams(0)
     send1(3)
-    grams(0)
+    grams(1)
     send2(2)
-    grams(1)
 
     def step(t):
         products = iterate(t)
@@ -302,11 +332,34 @@
             dma((CHUNKS,)),
             dma((CHUNKS,)),
         ],
-        compiler_params=pltpu.CompilerParams(collective_id=0, has_side_effects=True, vmem_limit_bytes=61000000),
+        compiler_params=pltpu.CompilerParams(collective_id=0, has_side_effects=True, vmem_limit_bytes=40 * 1024 * 1024),
         name="update",
     )(grad, moment, weight)
 
 
+def store(momentum, result, momentum_out, result_out, sems):
+    copies = [
+        pltpu.make_async_copy(momentum, momentum_out, sems.at[0]),
+        pltpu.make_async_copy(result, result_out, sems.at[1]),
+    ]
+    for copy in copies:
+        copy.start()
+    for copy in copies:
+        copy.wait()
+
+
+def put_out(momentum, result):
+    return pl.pallas_call(
+        store,
+        out_shape=[jax.ShapeDtypeStruct(momentum.shape, jnp.float32)] * 2,
+        in_specs=[pl.BlockSpec(memory_space=pltpu.VMEM)] * 2,
+        out_specs=[pl.BlockSpec(memory_space=pl.ANY)] * 2,
+        scratch_shapes=[pltpu.SemaphoreType.DMA((2,))],
+        compiler_params=pltpu.CompilerParams(vmem_limit_bytes=8 * 1024 * 1024),
+        name="put_out",
+    )(momentum, result)
+
+
 def tiles(a):
     return a.reshape(512, 4, 2, 128).transpose(0, 2, 1, 3).reshape(32, CHUNKS, 32, 128)
 
@@ -316,7 +369,8 @@
 
 
 def on_device(grad_stack, moment_stack, weight_stack):
-    momentum, result = update(tiles(grad_stack), tiles(moment_stack), tiles(weight_stack))
+    momentum, result = update(*[pltpu.with_memory_space_constraint(tiles(a), pltpu.HBM) for a in (grad_stack, moment_stack, weight_stack)])
+    momentum, result = put_out(momentum, result)
     return (untiled(result), untiled(momentum))
 
 

time: 68.1 us -> 60.4 us (0.89)
  local copies, waits for them, and re-layouts: 4.74 us -> 0 us
  Pallas kernels: 61.6 us -> 59.1 us
    unnamed x4 -> x0, local copies, waits for them, and re-layouts: 4.74 us -> none
    pallas_call x1, Pallas kernels: 61.6 us -> 57.1 us  [update(): pl.pallas_call(kernel, out_shape=[jax.ShapeDtypeStruct(whole, f32)] * 2,...]
    pallas_call x0 -> x1, Pallas kernels: none -> 2.03 us  [put_out(): pl.pallas_call(store, out_shape=[jax.ShapeDtypeStruct(momentum.shape, jnp...]
where the time goes in v3:
time: 60.4 us; the launch traced here: 59.7 us
  Pallas kernels  59.1 us (98%)
  between operations  0.64 us (1%)
    pallas_call x1, Pallas kernels, update(): pl.pallas_call(kernel, out_shape=[jax.ShapeDtypeStruct(whole, f32)] * 2,...  57.1 us
    pallas_call x1, Pallas kernels, put_out(): pl.pallas_call(store, out_shape=[jax.ShapeDtypeStruct(momentum.shape, jnp...  2.03 us

profile of v3, /device:TPU:0, one launch (start us, length us, event | category | flops | bytes accessed | tf_op | source)
XLA Modules:
  0.0 59.7 jit_solution(576077499411297598)
XLA Ops:
  0.6 57.1 %update.1 = (f32[32,4,32,128]{3,2,1,0:T(8,128)S(1)}, f32[32,4,32,128]{3,2,1,0:T(8,128)S(1)}) custom-call(f32[32,4,32,128]{3,2,1,0:T(8,128)} %bitcast.25, f32[32,4,32,128]{3,2,1,0:T(8,128)} %bitcast.26, f32[32,4,32,128]{3,2,1,0:T(8,128)} %bitcast.27), custom_call_target="tpu_custom_call" | custom-call | tf_op jit(solution)/shard_map/update/pallas_call | solution.py:307
  57.7 2.0 %put_out.1 = (f32[32,4,32,128]{3,2,1,0:T(8,128)}, f32[32,4,32,128]{3,2,1,0:T(8,128)}) custom-call(f32[32,4,32,128]{3,2,1,0:T(8,128)S(1)} %get-tuple-element.6.momentum, f32[32,4,32,128]{3,2,1,0:T(8,128)S(1)} %get-tuple-element.7.result), custom_call_target="tpu_custom_call" | custom-call | tf_op jit(solution)/shard_map/put_out/pallas_call | solution.py:352

commit v4 on v3

--- a/solution.py
+++ b/solution.py
@@ -12,6 +12,7 @@
 learn_rate = 1.0
 ITERS = 5
 CHUNKS = 4
+HUB = 2
 
 
 def split(a):
@@ -38,7 +39,7 @@
 def kernel(
     grad, moment, weight, momentum, result,
     gbuf, mbuf, wbuf, out1, in1, in2, zbuf, out2, in3, in4, gsend, gx,
-    load, wload, local, send, recv1, recv2, recv3, recv4, xrecv,
+    load, wload, local, send, recv1, recv2, recv3, recv4, xrecv, entered,
 ):
     row, col = lax.axis_index("rows"), lax.axis_index("cols")
     z, y = row // 4, row % 4
@@ -70,13 +71,22 @@
     def greet(device):
         pl.semaphore_signal(barrier, inc=1, device_id=device, device_id_type=MESH)
 
-    for chunk in range(CHUNKS):
+    def fetch(chunk):
         pltpu.make_async_copy(grad.at[:, chunk], gbuf.at[:, chunk], load.at[chunk]).start()
         pltpu.make_async_copy(moment.at[:, chunk], mbuf.at[:, chunk], load.at[CHUNKS + chunk]).start()
+
+    fetch(0)
+    for i in (5, 4, 3, 2, 7, 6):
+        for half in range(2):
+            greet(along_second(half, i)[2])
     greet({"rows": row, "cols": x * 2 + (core + 1) % 2})
-    loop(2, 8, lambda i: greet(along_second(0, i)[2]))
-    loop(2, 8, lambda i: greet(along_second(1, i)[2]))
-    loop(1, 4, lambda i: greet(x_peer(i)))
+
+    @pl.when(x != HUB)
+    def _():
+        greet({"rows": row, "cols": HUB * 2 + core})
+
+    for chunk in range(1, CHUNKS):
+        fetch(chunk)
 
     def remote(src, dst, sem, device, which):
         pltpu.make_async_remote_copy(
@@ -253,7 +263,17 @@
                 out2[chunk, half, 4 * k : 4 * k + 4] = jnp.concatenate([a, b], axis=1).reshape(4, 4, 16, 128)
 
     new_momentum(0)
-    pl.semaphore_wait(barrier, 16)
+
+    @pl.when(x != HUB)
+    def _():
+        pl.semaphore_wait(barrier, 13)
+
+    @pl.when(x == HUB)
+    def _():
+        pl.semaphore_wait(barrier, 16)
+        for i in (2, 1, 3):
+            pl.semaphore_signal(entered, inc=1, device_id=x_peer(i), device_id_type=MESH)
+
     send1(0)
     new_momentum(1)
     send1(1)
@@ -263,6 +283,11 @@
     send2(0)
     send2(1)
     send1(2)
+
+    @pl.when(x != HUB)
+    def _():
+        pl.semaphore_wait(entered, 1)
+
     grams(0)
     send1(3)
     grams(1)
@@ -331,6 +356,7 @@
             dma((CHUNKS,)),
             dma((CHUNKS,)),
             dma((CHUNKS,)),
+            pltpu.SemaphoreType.REGULAR,
         ],
         compiler_params=pltpu.CompilerParams(collective_id=0, has_side_effects=True, vmem_limit_bytes=40 * 1024 * 1024),
         name="update",
@@ -338,10 +364,11 @@
 
 
 def store(momentum, result, momentum_out, result_out, sems):
-    copies = [
-        pltpu.make_async_copy(momentum, momentum_out, sems.at[0]),
-        pltpu.make_async_copy(result, result_out, sems.at[1]),
-    ]
+    copies = []
+    for part in range(4):
+        at = pl.ds(8 * part, 8)
+        copies.append(pltpu.make_async_copy(momentum.at[at], momentum_out.at[at], sems.at[part]))
+        copies.append(pltpu.make_async_copy(result.at[at], result_out.at[at], sems.at[4 + part]))
     for copy in copies:
         copy.start()
     for copy in copies:
@@ -354,7 +381,7 @@
         out_shape=[jax.ShapeDtypeStruct(momentum.shape, jnp.float32)] * 2,
         in_specs=[pl.BlockSpec(memory_space=pltpu.VMEM)] * 2,
         out_specs=[pl.BlockSpec(memory_space=pl.ANY)] * 2,
-        scratch_shapes=[pltpu.SemaphoreType.DMA((2,))],
+        scratch_shapes=[pltpu.SemaphoreType.DMA((8,))],
         compiler_params=pltpu.CompilerParams(vmem_limit_bytes=8 * 1024 * 1024),
         name="put_out",
     )(momentum, result)

time: 60.4 us -> 59.8 us (0.990)
  Pallas kernels: 59.1 us -> 58.3 us
    pallas_call x1, Pallas kernels: 57.1 us -> 56.3 us  [update(): pl.pallas_call(kernel, out_shape=[jax.ShapeDtypeStruct(whole, f32)] * 2,...]
where the time goes in v4:
time: 59.8 us; the launch traced here: 59 us
  Pallas kernels  58.3 us (97%)
  between operations  0.64 us (1%)
    pallas_call x1, Pallas kernels, update(): pl.pallas_call(kernel, out_shape=[jax.ShapeDtypeStruct(whole, f32)] * 2,...  56.3 us
    pallas_call x1, Pallas kernels, put_out(): pl.pallas_call(store, out_shape=[jax.ShapeDtypeStruct(momentum.shape, jnp...  2.07 us

profile of v4, /device:TPU:0, one launch (start us, length us, event | category | flops | bytes accessed | tf_op | source)
XLA Modules:
  0.0 59.0 jit_solution(9082487981540993661)
XLA Ops:
  0.6 56.3 %update.1 = (f32[32,4,32,128]{3,2,1,0:T(8,128)S(1)}, f32[32,4,32,128]{3,2,1,0:T(8,128)S(1)}) custom-call(f32[32,4,32,128]{3,2,1,0:T(8,128)} %bitcast.25, f32[32,4,32,128]{3,2,1,0:T(8,128)} %bitcast.26, f32[32,4,32,128]{3,2,1,0:T(8,128)} %bitcast.27), custom_call_target="tpu_custom_call" | custom-call | tf_op jit(solution)/shard_map/update/pallas_call | solution.py:332
  56.9 2.1 %put_out.1 = (f32[32,4,32,128]{3,2,1,0:T(8,128)}, f32[32,4,32,128]{3,2,1,0:T(8,128)}) custom-call(f32[32,4,32,128]{3,2,1,0:T(8,128)S(1)} %get-tuple-element.6.momentum, f32[32,4,32,128]{3,2,1,0:T(8,128)S(1)} %get-tuple-element.7.result), custom_call_target="tpu_custom_call" | custom-call | tf_op jit(solution)/shard_map/put_out/pallas_call | solution.py:379

commit v5 on v4

--- a/solution.py
+++ b/solution.py
@@ -218,9 +218,9 @@
             even, odd = gram[:, 0], gram[:, 1]
             even, odd = even + roll4(even), odd + roll4(odd)
             gsend[chunk, 64 * half : 64 * half + 64, :] = jnp.where(low8, even, odd).reshape(64, 128)
+        gx[chunk, x] = gsend[chunk]
         for i in (2, 1, 3):
             remote(gsend.at[chunk], gx.at[chunk, x], xrecv.at[chunk], x_peer(i), 4)
-        gx[chunk, x] = gsend[chunk]
 
     def iterate(chunk):
         drain(gx.at[chunk, pl.ds(0, 3)], xrecv.at[chunk])
@@ -283,13 +283,13 @@
     send2(0)
     send2(1)
     send1(2)
+    send1(3)
 
     @pl.when(x != HUB)
     def _():
         pl.semaphore_wait(entered, 1)
 
     grams(0)
-    send1(3)
     grams(1)
     send2(2)
 
@@ -307,11 +307,12 @@
         def _():
             grams(t + 2)
 
-        @pl.when(t > 0)
+        @pl.when((t > 0) & (t < 3))
         def _():
             send4(t - 1)
 
     loop(0, CHUNKS, step)
+    send4(2)
     send4(3)
     pltpu.make_async_copy(weight, wbuf, wload).wait()
     loop(0, CHUNKS, subtract)

time: 59.8 us -> 59.7 us (level)
  no operation moved by 1% of the time
where the time goes in v5:
time: 59.7 us; the launch traced here: 58.9 us
  Pallas kernels  58.3 us (98%)
  between operations  0.64 us (1%)
    pallas_call x1, Pallas kernels, update(): pl.pallas_call(kernel, out_shape=[jax.ShapeDtypeStruct(whole, f32)] * 2,...  56.2 us
    pallas_call x1, Pallas kernels, put_out(): pl.pallas_call(store, out_shape=[jax.ShapeDtypeStruct(momentum.shape, jnp...  2.07 us

profile of v5, /device:TPU:0, one launch (start us, length us, event | category | flops | bytes accessed | tf_op | source)
XLA Modules:
  0.0 58.9 jit_solution(10704271917528823890)
XLA Ops:
  0.6 56.2 %update.1 = (f32[32,4,32,128]{3,2,1,0:T(8,128)S(1)}, f32[32,4,32,128]{3,2,1,0:T(8,128)S(1)}) custom-call(f32[32,4,32,128]{3,2,1,0:T(8,128)} %bitcast.25, f32[32,4,32,128]{3,2,1,0:T(8,128)} %bitcast.26, f32[32,4,32,128]{3,2,1,0:T(8,128)} %bitcast.27), custom_call_target="tpu_custom_call" | custom-call | tf_op jit(solution)/shard_map/update/pallas_call | solution.py:333
  56.8 2.1 %put_out.1 = (f32[32,4,32,128]{3,2,1,0:T(8,128)}, f32[32,4,32,128]{3,2,1,0:T(8,128)}) custom-call(f32[32,4,32,128]{3,2,1,0:T(8,128)S(1)} %get-tuple-element.6.momentum, f32[32,4,32,128]{3,2,1,0:T(8,128)S(1)} %get-tuple-element.7.result), custom_call_target="tpu_custom_call" | custom-call | tf_op jit(solution)/shard_map/put_out/pallas_call | solution.py:380

commit v6 on v5

--- a/solution.py
+++ b/solution.py
@@ -263,6 +263,7 @@
                 out2[chunk, half, 4 * k : 4 * k + 4] = jnp.concatenate([a, b], axis=1).reshape(4, 4, 16, 128)
 
     new_momentum(0)
+    new_momentum(1)
 
     @pl.when(x != HUB)
     def _():
@@ -271,12 +272,15 @@
     @pl.when(x == HUB)
     def _():
         pl.semaphore_wait(barrier, 16)
+
+    send1(0)
+    send1(1)
+
+    @pl.when(x == HUB)
+    def _():
         for i in (2, 1, 3):
             pl.semaphore_signal(entered, inc=1, device_id=x_peer(i), device_id_type=MESH)
 
-    send1(0)
-    new_momentum(1)
-    send1(1)
     new_momentum(2)
     new_momentum(3)
     pltpu.make_async_copy(weight, wbuf, wload).start()

time: 59.7 us -> 59.8 us (level)
  no operation moved by 1% of the time
where the time goes in v6:
time: 59.8 us; the launch traced here: 59 us
  Pallas kernels  58.3 us (97%)
  between operations  0.64 us (1%)
    pallas_call x1, Pallas kernels, update(): pl.pallas_call(kernel, out_shape=[jax.ShapeDtypeStruct(whole, f32)] * 2,...  56.2 us
    pallas_call x1, Pallas kernels, put_out(): pl.pallas_call(store, out_shape=[jax.ShapeDtypeStruct(momentum.shape, jnp...  2.07 us

profile of v6, /device:TPU:0, one launch (start us, length us, event | category | flops | bytes accessed | tf_op | source)
XLA Modules:
  0.0 59.0 jit_solution(4669983251549208422)
XLA Ops:
  0.6 56.2 %update.1 = (f32[32,4,32,128]{3,2,1,0:T(8,128)S(1)}, f32[32,4,32,128]{3,2,1,0:T(8,128)S(1)}) custom-call(f32[32,4,32,128]{3,2,1,0:T(8,128)} %bitcast.25, f32[32,4,32,128]{3,2,1,0:T(8,128)} %bitcast.26, f32[32,4,32,128]{3,2,1,0:T(8,128)} %bitcast.27), custom_call_target="tpu_custom_call" | custom-call | tf_op jit(solution)/shard_map/update/pallas_call | solution.py:337
  56.9 2.1 %put_out.1 = (f32[32,4,32,128]{3,2,1,0:T(8,128)}, f32[32,4,32,128]{3,2,1,0:T(8,128)}) custom-call(f32[32,4,32,128]{3,2,1,0:T(8,128)S(1)} %get-tuple-element.6.momentum, f32[32,4,32,128]{3,2,1,0:T(8,128)S(1)} %get-tuple-element.7.result), custom_call_target="tpu_custom_call" | custom-call | tf_op jit(solution)/shard_map/put_out/pallas_call | solution.py:384

commit v7 on v5

--- a/solution.py
+++ b/solution.py
@@ -283,13 +283,13 @@
     send2(0)
     send2(1)
     send1(2)
-    send1(3)
 
     @pl.when(x != HUB)
     def _():
         pl.semaphore_wait(entered, 1)
 
     grams(0)
+    send1(3)
     grams(1)
     send2(2)
 

time: 59.7 us -> 59.8 us (level)
  no operation moved by 1% of the time
where the time goes in v7:
time: 59.8 us; the launch traced here: 59 us
  Pallas kernels  58.3 us (97%)
  between operations  0.64 us (1%)
    pallas_call x1, Pallas kernels, update(): pl.pallas_call(kernel, out_shape=[jax.ShapeDtypeStruct(whole, f32)] * 2,...  56.3 us
    pallas_call x1, Pallas kernels, put_out(): pl.pallas_call(store, out_shape=[jax.ShapeDtypeStruct(momentum.shape, jnp...  2.07 us

profile of v7, /device:TPU:0, one launch (start us, length us, event | category | flops | bytes accessed | tf_op | source)
XLA Modules:
  0.0 59.0 jit_solution(2345006268383833214)
XLA Ops:
  0.6 56.3 %update.1 = (f32[32,4,32,128]{3,2,1,0:T(8,128)S(1)}, f32[32,4,32,128]{3,2,1,0:T(8,128)S(1)}) custom-call(f32[32,4,32,128]{3,2,1,0:T(8,128)} %bitcast.25, f32[32,4,32,128]{3,2,1,0:T(8,128)} %bitcast.26, f32[32,4,32,128]{3,2,1,0:T(8,128)} %bitcast.27), custom_call_target="tpu_custom_call" | custom-call | tf_op jit(solution)/shard_map/update/pallas_call | solution.py:333
  56.9 2.1 %put_out.1 = (f32[32,4,32,128]{3,2,1,0:T(8,128)}, f32[32,4,32,128]{3,2,1,0:T(8,128)}) custom-call(f32[32,4,32,128]{3,2,1,0:T(8,128)S(1)} %get-tuple-element.6.momentum, f32[32,4,32,128]{3,2,1,0:T(8,128)S(1)} %get-tuple-element.7.result), custom_call_target="tpu_custom_call" | custom-call | tf_op jit(solution)/shard_map/put_out/pallas_call | solution.py:380
